TPU v7x, 32 devices: a whole 2x2x4 slice. The times are simulated.
32 devices in a mesh: tile: 8 (over z, x), conv: 4 (over y, core).
Axes of the slice: x: 2, y: 2, z: 4, core: 2. Of those that a mesh axis runs over, the one named last changes fastest.
Arguments:
- field: float32 [256, 24576], P(None, ('tile', 'conv')), may hold values from -6 to 6
- interp: bfloat16 [32768, 384], P(('tile', 'conv')), may hold values from -0.1875 to 0.1875
- conv_blocks: bfloat16 [64, 3, 256, 256], P(('tile', 'conv')), may hold values from -0.21875 to 0.21875
- band_shift: int32 [64, 3], P(('tile', 'conv')), may hold values from 0 to 1
- owner: int32 [12288, 1], P(('tile', 'conv')), may hold values from 0 to 3; in each aligned block of 384 rows (0 to 383, 384 to 767, ...) at most 128 rows name the same one
- edge_index: int32 [64, 128], P(('tile', 'conv')), may hold values from 0 to 767, as said below
Outputs:
- correlated: float32 [256, 24576], P(None, ('tile', 'conv'))
Inputs may be any that keep to these rules, and one draw needn't show every extreme that they name: `edge_index`: row 2b lists the first 128 columns of domain b in some order, row 2b + 1 its last 128 columns in some order. Among the 384 points of one domain no owner is named more than 128 times, and in some domains one owner is named exactly 128 times.
All inputs are finite; a program needn't handle non-finite values.
Results may differ from a plain program's by a relative error of at most 0.0049.
Values may be sent and summed in bfloat16 or wider, within the bound.
A program may use at most 64 MiB of HBM per device.

v0:
```python
import jax
import jax.numpy as jnp
from jax import lax
from jax.sharding import PartitionSpec as P


def padded(cells, sides, width):
    for axis, dim in sides:
        count = lax.axis_size(axis)
        head = lax.slice_in_dim(cells, 0, width, axis=dim)
        tail = lax.slice_in_dim(cells, cells.shape[dim] - width, cells.shape[dim], axis=dim)
        cells = jnp.concatenate(
            [
                lax.ppermute(tail, axis, [(i, (i + 1) % count) for i in range(count)]),
                cells,
                lax.ppermute(head, axis, [((i + 1) % count, i) for i in range(count)]),
            ],
            axis=dim,
        )
    return cells


def contract_last(left_side, right_side):
    return lax.dot_general(
        left_side, right_side, (((1,), (1,)), ((), ())), preferred_element_type=jnp.float32
    )


def convolve(values, conv_blocks, band_shift):
    height = values.shape[0]
    owned_blocks = conv_blocks.shape[0]
    points = conv_blocks.shape[2]
    pieces = values.reshape(height, owned_blocks, points)
    source = (jnp.arange(owned_blocks, dtype=jnp.int32)[:, None] + band_shift) % owned_blocks
    select = (
        source[:, :, None] == jnp.arange(owned_blocks, dtype=jnp.int32)[None, None, :]
    ).astype(jnp.bfloat16)
    picked = jnp.einsum("rsp,jbs->rjbp", pieces, select, preferred_element_type=jnp.float32).astype(
        jnp.bfloat16
    )
    forward = jnp.einsum(
        "rjbp,jbpq->rjq", picked, conv_blocks, preferred_element_type=jnp.float32
    ).astype(jnp.bfloat16)
    backward = jnp.einsum(
        "rjq,jbpq->rjbp", forward, conv_blocks, preferred_element_type=jnp.float32
    )
    adjoint = jnp.einsum(
        "rjbp,jbs->rsp", backward, select.astype(jnp.float32), precision=lax.Precision.HIGHEST
    )
    return adjoint.reshape(height, owned_blocks * points).astype(jnp.bfloat16)


def on_device(field, interp, conv_blocks, band_shift, owner, edge_index):
    columns = field.shape[1]
    rim_width = edge_index.shape[1]
    groups = lax.axis_size("conv")
    slot_count = conv_blocks.shape[0] * conv_blocks.shape[2]
    capacity = slot_count // groups
    rounded = field.astype(jnp.bfloat16)
    left_list = edge_index[0]
    right_list = edge_index[1]
    rim_values = jnp.concatenate(
        [jnp.take(rounded, left_list, axis=1), jnp.take(rounded, right_list, axis=1)], axis=1
    )
    widened = padded(rim_values, ((("tile", "conv"), 1),), rim_width)
    from_left = widened[:, :rim_width]
    from_right = widened[:, 3 * rim_width :]
    extended = jnp.concatenate([from_left, rounded, from_right], axis=1)
    subgrid = jnp.dot(extended, interp, preferred_element_type=jnp.float32)
    subgrid = subgrid.astype(jnp.bfloat16)
    owners = owner[:, 0]
    choose = (owners[:, None] == jnp.arange(groups, dtype=jnp.int32)[None, :]).astype(jnp.int32)
    before = jnp.cumsum(choose, axis=0) - choose
    position = jnp.sum(before * choose, axis=1)
    slot_index = owners * capacity + position
    placement = (slot_index[:, None] == jnp.arange(slot_count, dtype=jnp.int32)[None, :]).astype(
        jnp.bfloat16
    )
    outgoing = jnp.dot(subgrid, placement, preferred_element_type=jnp.float32).astype(jnp.bfloat16)
    incoming = lax.all_to_all(
        convolve(
            lax.all_to_all(outgoing, "conv", split_axis=1, concat_axis=1, tiled=True),
            conv_blocks,
            band_shift,
        ),
        "conv",
        split_axis=1,
        concat_axis=1,
        tiled=True,
    )
    returned = contract_last(incoming, placement).astype(jnp.bfloat16)
    partial_value = contract_last(returned, interp)
    left_part = partial_value[:, :rim_width]
    right_part = partial_value[:, rim_width + columns :]
    edge_sums = padded(
        jnp.concatenate([left_part, right_part], axis=1).astype(jnp.bfloat16),
        ((("tile", "conv"), 1),),
        rim_width,
    ).astype(jnp.float32)
    interior_part = partial_value[:, rim_width : rim_width + columns]
    result = interior_part.at[:, left_list].add(edge_sums[:, :rim_width])
    result = result.at[:, right_list].add(edge_sums[:, 3 * rim_width :])
    return result


def solution(mesh):
    return jax.shard_map(
        on_device,
        mesh=mesh,
        in_specs=(
            P(None, ("tile", "conv")),
            P(("tile", "conv"), None),
            P(("tile", "conv"), None, None, None),
            P(("tile", "conv"), None),
            P(("tile", "conv"), None),
            P(("tile", "conv"), None),
        ),
        out_specs=P(None, ("tile", "conv")),
        check_vma=False,
    )
```

profile of v0, /device:TPU:0, one launch (start us, length us, event | category | flops | bytes accessed | tf_op | source)
XLA Modules:
  0.0 51.1 jit_solution(18035988229664410516)
XLA Ops:
  0.0 0.0 copy-start
  0.0 0.0 copy-start.1
  0.0 0.8 %compare_and_fusion.1 = (pred[128]{0:T(512)(128)(4,1)S(1)}, s32[128]{0:T(128)S(1)}, pred[128]{0:T(512)(128)(4,1)S(1)}, s32[128]{0:T(128)S(1)}) fusion(s32[2,128]{1,0:T(2,128)} %param.13), kind=kLoop, calls=%fused_computation.58 | loop fusion | flops 1536 | bytes 2304 | tf_op jit(solution)/shard_map/jit(_take)/and | solution.py:63
  0.8 1.3 %copy.27 = bf16[256,768]{0,1:T(8,128)(2,1)S(1)} copy(f32[256,768]{1,0:T(8,128)} %param.8) | data formatting | bytes 1179648 | tf_op args[0]
  2.1 0.8 %gather_fusion = bf16[128,256]{1,0:T(8,128)(2,1)S(1)} fusion(bf16[256,768]{0,1:T(8,128)(2,1)S(1)} %copy.27, s32[1024]{0:T(1024)S(1)} %pad_clamp_fusion.1), kind=kCustom, calls=%fused_computation.clone | custom fusion | bytes 131584 | tf_op jit(solution)/shard_map/jit(_take)/gather | solution.py:63
  3.0 0.1 select_bitcast_fusion.1
  3.1 0.5 %collective-permute-start = (bf16[256,128]{0,1:T(8,128)(2,1)S(1)}, bf16[256,128]{0,1:T(8,128)(2,1)S(1)}, u32[]{:S(2)}, u32[]{:S(2)}) collective-permute-start(bf16[256,128]{0,1:T(8,128)(2,1)S(1)} %select_bitcast_fusion.1), channel_id=1, source_target_pairs={{0,1},{1,2},{2,3},{3,4},{4,5},{5,6},{6,7},{7,8},{8,9},{9,10},{10,1... | collective-permute-start | bytes 196616 | tf_op jit(solution)/shard_map/ppermute | solution.py:14
  3.6 0.8 %gather_fusion.1 = bf16[128,256]{1,0:T(8,128)(2,1)S(1)} fusion(bf16[256,768]{0,1:T(8,128)(2,1)S(1)} %copy.27, s32[1024]{0:T(1024)S(1)} %pad_clamp_fusion), kind=kCustom, calls=%fused_computation.1.clone | custom fusion | bytes 131584 | tf_op jit(solution)/shard_map/jit(_take)/gather | solution.py:63
  4.5 0.1 select_bitcast_fusion
  4.5 6.0 %collective-permute-start.1 = (bf16[256,128]{0,1:T(8,128)(2,1)S(1)}, bf16[256,128]{0,1:T(8,128)(2,1)S(1)}, u32[]{:S(2)}, u32[]{:S(2)}) collective-permute-start(bf16[256,128]{0,1:T(8,128)(2,1)S(1)} %select_bitcast_fusion), channel_id=1, source_target_pairs={{1,0},{2,1},{3,2},{4,3},{5,4},{6,5},{7,6},{8,7},{9,8},{10,9},{11,1... | collective-permute-start | bytes 196616 | tf_op jit(solution)/shard_map/ppermute | solution.py:16
  10.5 0.0 copy-done.1
  10.6 1.2 %reduce-window.6 = s32[4,3,128]{2,1,0:T(4,128)S(1)} reduce-window(s32[4,3,128]{2,1,0:T(4,128)S(1)} %fusion.32, s32[]{:T(128)} %constant.30.clone.1), window={size=1x1x128 pad=0_0x0_0x127_0}, to_apply=%region_0.0 | reduce-window | flops 195072 | bytes 12292 | tf_op jit(solution)/shard_map/reduce-window
  11.8 0.2 slice_reduce_fusion
  12.0 0.2 reduce-window.9
  12.2 0.1 add_bitcast_fusion
  12.3 0.0 copy-start.3
  12.3 0.0 collective-permute-done
  12.3 0.1 collective-permute-done.1
  12.4 0.0 copy-done
  12.4 0.7 %fusion.10 = bf16[32,4,8,128]{3,2,1,0:T(8,128)(2,1)S(1)} fusion(bf16[1024,384]{1,0:T(8,128)(2,1)S(1)} %copy-done, bf16[256,128]{0,1:T(8,128)(2,1)S(1)} %collective-permute-done.1, bf16[256,768]{0,1:T(8,128)(2,1)S(1)} %copy.27, bf16[256,128]{0,1:T(8,128)(2,1)S(1)} %collective-permute-done, s32[384]{0:T(512)S(1)} %add_reduce_fusion), kind=kOutput, calls=%fused_computation.16 | convolution fusion | flops 303988736 | bytes 1574400 | tf_op jit(solution)/shard_map/dot_general | solution.py:79
  13.1 0.7 %copy.58 = bf16[32,4,8,128]{3,2,0,1:T(8,128)(2,1)} copy(bf16[32,4,8,128]{3,2,1,0:T(8,128)(2,1)S(1)} %fusion.10) | data formatting | bytes 524288 | tf_op jit(solution)/shard_map/all_to_all | solution.py:82
  13.9 3.4 %all-to-all-start = ((bf16[256,4,128]{2,0,1:T(8,128)(2,1)}), bf16[256,4,128]{2,0,1:T(8,128)(2,1)S(1)}, u32[]{:S(2)}, u32[]{:S(2)}) async-start(bf16[256,4,128]{2,0,1:T(8,128)(2,1)} %bitcast.89), calls=%async_computation | async-start | bytes 524288 | tf_op jit(solution)/shard_map/all_to_all | solution.py:82
  17.3 0.0 copy-done.3
  17.3 5.9 %all-to-all-done = bf16[256,4,128]{2,0,1:T(8,128)(2,1)S(1)} async-done(((bf16[256,4,128]{2,0,1:T(8,128)(2,1)}), bf16[256,4,128]{2,0,1:T(8,128)(2,1)S(1)}, u32[]{:S(2)}, u32[]{:S(2)}) %all-to-all-start) | async-done | bytes 262176 | tf_op jit(solution)/shard_map/all_to_all | solution.py:82
  23.3 0.2 copy.29
  23.5 0.2 reshape.131
  23.7 1.0 %fusion.2 = bf16[256,2,3,256]{3,2,0,1:T(4,128)(2,1)S(1)} fusion(bf16[256,2,256,1]{2,1,0,3:T(2,128)(2,1)S(1)} %reshape.131, s32[2,3]{1,0:T(2,128)S(1)} %and_select_fusion), kind=kOutput, calls=%fused_computation.8 | convolution fusion | flops 1966092 | bytes 1048600 | tf_op jit(solution)/shard_map/rsp,jbs->rjbp/dot_general | solution.py:38
  24.7 2.0 %convolution_bitcast_fusion = f32[256,2,3,256]{3,0,2,1:T(8,128)S(1)} fusion(bf16[2,3,256,256]{3,2,1,0:T(8,128)(2,1)} %param.10, bf16[256,2,3,256]{3,2,0,1:T(4,128)(2,1)S(1)} %fusion.2), kind=kOutput, calls=%fused_computation.6 | convolution fusion | flops 402784256 | bytes 3145728 | tf_op jit(solution)/shard_map/rjq,jbpq->rjbp/dot_general | solution.py:44
  26.7 2.9 %fusion.11 = bf16[256,2,256]{2,1,0:T(2,128)(2,1)S(1)} fusion(f32[256,2,3,256]{3,0,2,1:T(8,128)S(1)} %convolution_bitcast_fusion, s32[2,3]{1,0:T(2,128)S(1)} %and_select_fusion), kind=kOutput, calls=%fused_computation.17 | convolution fusion | flops 9568268 | bytes 1835032 | tf_op jit(solution)/shard_map/rjbp,jbs->rsp/dot_general | solution.py:47
  29.6 0.2 convert_element_type.59
  29.9 8.4 %all_to_all.18 = bf16[256,4,128]{2,0,1:T(8,128)(2,1)S(1)} all-to-all(bf16[256,4,128]{2,0,1:T(8,128)(2,1)S(1)} %copy.32), channel_id=1, replica_groups=mesh['tile'=8,'conv'=4] {'conv'}, dimensions={1} | all-to-all | bytes 524288 | tf_op jit(solution)/shard_map/all_to_all | solution.py:80
  38.3 0.1 copy.33
  38.4 0.0 copy-start.2
  38.4 0.8 %fusion.46 = (bf16[256,1024]{1,0:T(8,128)(2,1)S(1)}, f32[256,1024]{1,0:T(8,128)S(1)}) fusion(bf16[1024,384]{1,0:T(8,128)(2,1)S(1)} %copy-done, bf16[256,512]{0,1:T(8,128)(2,1)S(1)} %bitcast.91, s32[384]{0:T(512)S(1)} %add_reduce_fusion), kind=kOutput, calls=%fused_computation.68 | convolution fusion | flops 302546944 | bytes 2622976 | tf_op jit(solution)/shard_map/dot_general | solution.py:24
  39.2 0.1 collective-permute-start.2
  39.3 5.3 %collective-permute-start.3 = (bf16[256,128]{1,0:T(8,128)(2,1)S(1)}, bf16[256,128]{1,0:T(8,128)(2,1)S(1)}, u32[]{:S(2)}, u32[]{:S(2)}) collective-permute-start(bf16[256,128]{1,0:T(8,128)(2,1)S(1)} %get-tuple-element.11), channel_id=1, source_target_pairs={{1,0},{2,1},{3,2},{4,3},{5,4},{6,5},{7,6},{8,7},{9,8},{10,9},{11,1... | collective-permute-start | bytes 196616 | tf_op jit(solution)/shard_map/ppermute | solution.py:16
  44.6 0.0 copy-done.2
  44.6 0.1 slice.45
  44.7 0.3 copy.34
  45.0 1.6 %collective-permute-done.2 = bf16[256,128]{1,0:T(8,128)(2,1)S(1)} collective-permute-done((bf16[256,128]{1,0:T(8,128)(2,1)S(1)}, bf16[256,128]{1,0:T(8,128)(2,1)S(1)}, u32[]{:S(2)}, u32[]{:S(2)}) %collective-permute-start.2) | collective-permute-done | bytes 65568 | tf_op jit(solution)/shard_map/ppermute | solution.py:14
  46.6 0.0 collective-permute-done.3
  46.6 0.1 copy.35
  46.7 0.1 copy.36
  46.8 1.6 %scatter_fusion = f32[256,768]{0,1:T(8,128)S(1)} fusion(f32[256,768]{0,1:T(8,128)S(1)} %copy.34, s32[128]{0:T(128)S(1)} %get-tuple-element.15, f32[128,256]{1,0:T(8,128)S(1)} %copy.35), kind=kCustom, calls=%fused_computation.2 | custom fusion | flops 32768 | bytes 393728 | tf_op jit(solution)/shard_map/scatter-add | solution.py:101
  48.4 1.6 %scatter_fusion.1 = f32[256,768]{0,1:T(8,128)S(1)} fusion(f32[256,768]{0,1:T(8,128)S(1)} %scatter_fusion, s32[128]{0:T(128)S(1)} %get-tuple-element.14, f32[128,256]{1,0:T(8,128)S(1)} %copy.36), kind=kCustom, calls=%fused_computation.3 | custom fusion | flops 32768 | bytes 393728 | tf_op jit(solution)/shard_map/scatter-add | solution.py:102
  50.0 1.1 %copy.37 = f32[256,768]{1,0:T(8,128)} copy(f32[256,768]{0,1:T(8,128)S(1)} %scatter_fusion.1) | data formatting | bytes 1572864 | tf_op jit(solution)/shard_map/scatter-add | solution.py:102
  (11 shorter events, 0.2 us)
Async XLA Ops:
  0.0 12.4 %copy-start = (bf16[1024,384]{1,0:T(8,128)(2,1)S(1)}, bf16[1024,384]{1,0:T(8,128)(2,1)}, u32[]{:S(2)}) copy-start(bf16[1024,384]{1,0:T(8,128)(2,1)} %param.9) | copy-start | bytes 2359300
  0.0 10.5 %copy-start.1 = (s32[384,1]{0,1:T(1,128)S(1)}, s32[384,1]{0,1:T(1,128)}, u32[]{:S(2)}) copy-start(s32[384,1]{0,1:T(1,128)} %param.12) | copy-start | bytes 4612
  3.1 9.3 %collective-permute-start = (bf16[256,128]{0,1:T(8,128)(2,1)S(1)}, bf16[256,128]{0,1:T(8,128)(2,1)S(1)}, u32[]{:S(2)}, u32[]{:S(2)}) collective-permute-start(bf16[256,128]{0,1:T(8,128)(2,1)S(1)} %select_bitcast_fusion.1), channel_id=1, source_target_pairs={{0,1},{1,2},{2,3},{3,4},{4,5},{5,6},{6,7},{7,8},{8,9},{9,10},{10,1... | collective-permute-start | bytes 196616 | tf_op jit(solution)/shard_map/ppermute | solution.py:14
  4.5 7.9 %collective-permute-start.1 = (bf16[256,128]{0,1:T(8,128)(2,1)S(1)}, bf16[256,128]{0,1:T(8,128)(2,1)S(1)}, u32[]{:S(2)}, u32[]{:S(2)}) collective-permute-start(bf16[256,128]{0,1:T(8,128)(2,1)S(1)} %select_bitcast_fusion), channel_id=1, source_target_pairs={{1,0},{2,1},{3,2},{4,3},{5,4},{6,5},{7,6},{8,7},{9,8},{10,9},{11,1... | collective-permute-start | bytes 196616 | tf_op jit(solution)/shard_map/ppermute | solution.py:16
  12.3 5.0 %copy-start.3 = (s32[2,3]{1,0:T(2,128)S(1)}, s32[2,3]{1,0:T(2,128)}, u32[]{:S(2)}) copy-start(s32[2,3]{1,0:T(2,128)} %param.11) | copy-start | bytes 76
  13.9 9.4 %all-to-all-start = ((bf16[256,4,128]{2,0,1:T(8,128)(2,1)}), bf16[256,4,128]{2,0,1:T(8,128)(2,1)S(1)}, u32[]{:S(2)}, u32[]{:S(2)}) async-start(bf16[256,4,128]{2,0,1:T(8,128)(2,1)} %bitcast.89), calls=%async_computation | async-start | bytes 524288 | tf_op jit(solution)/shard_map/all_to_all | solution.py:82
  38.4 6.2 %copy-start.2 = (s32[2,128]{1,0:T(2,128)S(1)}, s32[2,128]{1,0:T(2,128)}, u32[]{:S(2)}) copy-start(s32[2,128]{1,0:T(2,128)} %param.13) | copy-start | bytes 3076
  39.2 7.3 %collective-permute-start.2 = (bf16[256,128]{1,0:T(8,128)(2,1)S(1)}, bf16[256,128]{1,0:T(8,128)(2,1)S(1)}, u32[]{:S(2)}, u32[]{:S(2)}) collective-permute-start(bf16[256,128]{1,0:T(8,128)(2,1)S(1)} %get-tuple-element.10), channel_id=1, source_target_pairs={{0,1},{1,2},{2,3},{3,4},{4,5},{5,6},{6,7},{7,8},{8,9},{9,10},{10,1... | collective-permute-start | bytes 196616 | tf_op jit(solution)/shard_map/ppermute | solution.py:14
  39.3 7.3 %collective-permute-start.3 = (bf16[256,128]{1,0:T(8,128)(2,1)S(1)}, bf16[256,128]{1,0:T(8,128)(2,1)S(1)}, u32[]{:S(2)}, u32[]{:S(2)}) collective-permute-start(bf16[256,128]{1,0:T(8,128)(2,1)S(1)} %get-tuple-element.11), channel_id=1, source_target_pairs={{1,0},{2,1},{3,2},{4,3},{5,4},{6,5},{7,6},{8,7},{9,8},{10,9},{11,1... | collective-permute-start | bytes 196616 | tf_op jit(solution)/shard_map/ppermute | solution.py:16
where the time goes:
time: 51.4 us; the launch traced here: 51.1 us
  starting transfers between devices  15.3 us (30%)
  blocking collectives  8.39 us (16%)
  waiting for transfers between devices  7.66 us (15%)
  matrix products  7.43 us (14%)
  local copies, waits for them, and re-layouts  6.38 us (12%)
  other arithmetic  5.73 us (11%)
    ppermute x2, starting transfers between devices, padded(): lax.ppermute(head, axis, [((i + 1) % count, i) for i in range(count)])  11.3 us
    all_to_all x1, blocking collectives, on_device(): lax.all_to_all(convolve(lax.all_to_all(outgoing, 'conv', split_axis=1, co...  8.39 us
    all_to_all x1, waiting for transfers between devices, on_device(): lax.all_to_all(outgoing, 'conv', split_axis=1, concat_axis=1, tiled=True)  5.95 us
    all_to_all x1, starting transfers between devices, on_device(): lax.all_to_all(outgoing, 'conv', split_axis=1, concat_axis=1, tiled=True)  3.41 us
    dot_general x1, matrix products, convolve(): jnp.einsum('rjbp,jbs->rsp', backward, select.astype(jnp.float32), precisi...  2.94 us
    dot_general x1, matrix products, convolve(): jnp.einsum('rjq,jbpq->rjbp', forward, conv_blocks, preferred_element_type...  2.02 us
    ppermute x2, waiting for transfers between devices, padded(): lax.ppermute(tail, axis, [(i, (i + 1) % count) for i in range(count)])  1.61 us
    scatter-add x1, other arithmetic, on_device(): result = interior_part.at[:, left_list].add(edge_sums[:, :rim_width])  1.59 us
  transfers between devices with their start and end apart: 5, of which 3 were waited for; matrix products, arithmetic and copies ran while one was open for 6% of the time, Pallas kernels for 0%

commit v1 on v0

--- a/solution.py
+++ b/solution.py
@@ -2,6 +2,29 @@
 import jax.numpy as jnp
 from jax import lax
 from jax.sharding import PartitionSpec as P
+
+
+def in_blocks(shard, dim, length):
+    lengths = shard.shape
+    tiles = shard.reshape(*lengths[:dim], length, lengths[dim] // length, *lengths[dim + 1 :])
+    return jnp.moveaxis(tiles, dim, 0)
+
+
+def in_order(pieces, dim):
+    pieces = jnp.moveaxis(pieces, 0, dim)
+    shape = pieces.shape
+    return pieces.reshape(*shape[:dim], shape[dim] * shape[dim + 1], *shape[dim + 2 :])
+
+
+def swapped_with_each(value, axis, split_dim, concat_dim):
+    devices, mine = (lax.axis_size(axis), lax.axis_index(axis))
+    blocks = in_blocks(value, split_dim, devices)
+    outs = [blocks[mine]]
+    for step in range(1, devices):
+        sent = blocks[mine ^ step]
+        outs.append(lax.ppermute(sent, axis, [(i, i ^ step) for i in range(devices)]))
+    blocks = jnp.stack(outs)[mine ^ jnp.arange(devices)]
+    return in_order(blocks, concat_dim)
 
 
 def padded(cells, sides, width):
@@ -77,16 +100,15 @@
         jnp.bfloat16
     )
     outgoing = jnp.dot(subgrid, placement, preferred_element_type=jnp.float32).astype(jnp.bfloat16)
-    incoming = lax.all_to_all(
+    incoming = swapped_with_each(
         convolve(
             lax.all_to_all(outgoing, "conv", split_axis=1, concat_axis=1, tiled=True),
             conv_blocks,
             band_shift,
         ),
         "conv",
-        split_axis=1,
-        concat_axis=1,
-        tiled=True,
+        1,
+        1,
     )
     returned = contract_last(incoming, placement).astype(jnp.bfloat16)
     partial_value = contract_last(returned, interp)

time: 51.4 us -> 49.8 us (0.969)
  blocking collectives: 8.39 us -> 0 us
  waiting for transfers between devices: 7.66 us -> 11.1 us
  starting transfers between devices: 15.3 us -> 17.4 us
  local copies, waits for them, and re-layouts: 6.38 us -> 7.54 us
    all_to_all x1 -> x0, blocking collectives: 8.39 us -> none  [on_device(): lax.all_to_all(convolve(lax.all_to_all(outgoing, 'conv', split_axis=1, co...]
    ppermute x0 -> x3, waiting for transfers between devices: none -> 3.46 us  [swapped_with_each(): lax.ppermute(sent, axis, [(i, i ^ step) for i in range(devices)])]
    ppermute x0 -> x3, starting transfers between devices: none -> 2.04 us  [swapped_with_each(): lax.ppermute(sent, axis, [(i, i ^ step) for i in range(devices)])]
    gather x0 -> x1, local copies, waits for them, and re-layouts: none -> 0.6 us  [swapped_with_each(): blocks = jnp.stack(outs)[mine ^ jnp.arange(devices)]]
    another operation x0 -> x1, local copies, waits for them, and re-layouts: none -> 0.55 us
    unnamed x9 -> x13, local copies, waits for them, and re-layouts: 1.32 us -> 1.37 us
    another operation x2 -> x3, other arithmetic: 1.4 us -> 1.44 us
  transfers between devices with their start and end apart: 5 -> 8, of which waited for: 3 -> 5; matrix products, arithmetic and copies ran while one was open for 6% -> 6% of each run, Pallas kernels for 0% -> 0%
where the time goes in v1:
time: 49.8 us; the launch traced here: 49.5 us
  starting transfers between devices  17.4 us (35%)
  waiting for transfers between devices  11.1 us (22%)
  local copies, waits for them, and re-layouts  7.54 us (15%)
  matrix products  7.44 us (15%)
  other arithmetic  5.78 us (12%)
    ppermute x2, starting transfers between devices, padded(): lax.ppermute(head, axis, [((i + 1) % count, i) for i in range(count)])  11 us
    all_to_all x1, waiting for transfers between devices, on_device(): lax.all_to_all(outgoing, 'conv', split_axis=1, concat_axis=1, tiled=True)  5.95 us
    ppermute x3, waiting for transfers between devices, swapped_with_each(): lax.ppermute(sent, axis, [(i, i ^ step) for i in range(devices)])  3.46 us
    all_to_all x1, starting transfers between devices, on_device(): lax.all_to_all(outgoing, 'conv', split_axis=1, concat_axis=1, tiled=True)  3.41 us
    dot_general x1, matrix products, convolve(): jnp.einsum('rjbp,jbs->rsp', backward, select.astype(jnp.float32), precisi...  2.94 us
    ppermute x3, starting transfers between devices, swapped_with_each(): lax.ppermute(sent, axis, [(i, i ^ step) for i in range(devices)])  2.04 us
    dot_general x1, matrix products, convolve(): jnp.einsum('rjq,jbpq->rjbp', forward, conv_blocks, preferred_element_type...  2.02 us
    ppermute x2, waiting for transfers between devices, padded(): lax.ppermute(tail, axis, [(i, (i + 1) % count) for i in range(count)])  1.61 us
  transfers between devices with their start and end apart: 8, of which 5 were waited for; matrix products, arithmetic and copies ran while one was open for 6% of the time, Pallas kernels for 0%

profile of v1, /device:TPU:0, one launch (start us, length us, event | category | flops | bytes accessed | tf_op | source)
XLA Modules:
  0.0 49.5 jit_solution(12062524775466962012)
XLA Ops:
  0.0 0.0 copy-start
  0.0 0.0 copy-start.1
  0.0 0.8 %compare_and_fusion.1 = (pred[128]{0:T(512)(128)(4,1)S(1)}, s32[128]{0:T(128)S(1)}, pred[128]{0:T(512)(128)(4,1)S(1)}, s32[128]{0:T(128)S(1)}) fusion(s32[2,128]{1,0:T(2,128)} %param.13), kind=kLoop, calls=%fused_computation.66 | loop fusion | flops 1536 | bytes 2304 | tf_op jit(solution)/shard_map/jit(_take)/and | solution.py:86
  0.8 1.3 %copy.22 = bf16[256,768]{0,1:T(8,128)(2,1)S(1)} copy(f32[256,768]{1,0:T(8,128)} %param.8) | data formatting | bytes 1179648 | tf_op args[0]
  2.1 0.8 %gather_fusion.1 = bf16[128,256]{1,0:T(8,128)(2,1)S(1)} fusion(bf16[256,768]{0,1:T(8,128)(2,1)S(1)} %copy.22, s32[1024]{0:T(1024)S(1)} %pad_clamp_fusion.2), kind=kCustom, calls=%fused_computation.clone | custom fusion | bytes 131584 | tf_op jit(solution)/shard_map/jit(_take)/gather | solution.py:86
  3.0 0.1 select_bitcast_fusion.1
  3.1 0.5 %collective-permute-start = (bf16[256,128]{0,1:T(8,128)(2,1)S(1)}, bf16[256,128]{0,1:T(8,128)(2,1)S(1)}, u32[]{:S(2)}, u32[]{:S(2)}) collective-permute-start(bf16[256,128]{0,1:T(8,128)(2,1)S(1)} %select_bitcast_fusion.1), channel_id=1, source_target_pairs={{0,1},{1,2},{2,3},{3,4},{4,5},{5,6},{6,7},{7,8},{8,9},{9,10},{10,1... | collective-permute-start | bytes 196616 | tf_op jit(solution)/shard_map/ppermute | solution.py:37
  3.6 0.8 %gather_fusion.2 = bf16[128,256]{1,0:T(8,128)(2,1)S(1)} fusion(bf16[256,768]{0,1:T(8,128)(2,1)S(1)} %copy.22, s32[1024]{0:T(1024)S(1)} %pad_clamp_fusion.1), kind=kCustom, calls=%fused_computation.1.clone | custom fusion | bytes 131584 | tf_op jit(solution)/shard_map/jit(_take)/gather | solution.py:86
  4.5 0.1 select_bitcast_fusion
  4.5 6.0 %collective-permute-start.1 = (bf16[256,128]{0,1:T(8,128)(2,1)S(1)}, bf16[256,128]{0,1:T(8,128)(2,1)S(1)}, u32[]{:S(2)}, u32[]{:S(2)}) collective-permute-start(bf16[256,128]{0,1:T(8,128)(2,1)S(1)} %select_bitcast_fusion), channel_id=1, source_target_pairs={{1,0},{2,1},{3,2},{4,3},{5,4},{6,5},{7,6},{8,7},{9,8},{10,9},{11,1... | collective-permute-start | bytes 196616 | tf_op jit(solution)/shard_map/ppermute | solution.py:39
  10.5 0.0 copy-done.1
  10.6 1.2 %reduce-window.6 = s32[4,3,128]{2,1,0:T(4,128)S(1)} reduce-window(s32[4,3,128]{2,1,0:T(4,128)S(1)} %fusion.32, s32[]{:T(128)} %constant.16.clone.1), window={size=1x1x128 pad=0_0x0_0x127_0}, to_apply=%region_0.0 | reduce-window | flops 195072 | bytes 12292 | tf_op jit(solution)/shard_map/reduce-window
  11.8 0.2 slice_reduce_fusion
  12.0 0.2 reduce-window.9
  12.2 0.1 add_bitcast_fusion
  12.3 0.0 copy-start.3
  12.3 0.0 collective-permute-done
  12.4 0.1 collective-permute-done.1
  12.4 0.0 copy-done
  12.4 0.7 %fusion.10 = bf16[32,4,8,128]{3,2,1,0:T(8,128)(2,1)S(1)} fusion(bf16[1024,384]{1,0:T(8,128)(2,1)S(1)} %copy-done, bf16[256,128]{0,1:T(8,128)(2,1)S(1)} %collective-permute-done.1, bf16[256,768]{0,1:T(8,128)(2,1)S(1)} %copy.22, bf16[256,128]{0,1:T(8,128)(2,1)S(1)} %collective-permute-done, s32[384]{0:T(512)S(1)} %add_reduce_fusion), kind=kOutput, calls=%fused_computation.17 | convolution fusion | flops 303988736 | bytes 1574400 | tf_op jit(solution)/shard_map/dot_general | solution.py:102
  13.1 0.7 %copy.64 = bf16[32,4,8,128]{3,2,0,1:T(8,128)(2,1)} copy(bf16[32,4,8,128]{3,2,1,0:T(8,128)(2,1)S(1)} %fusion.10) | data formatting | bytes 524288 | tf_op jit(solution)/shard_map/all_to_all | solution.py:105
  13.9 3.4 %all-to-all-start = ((bf16[256,4,128]{2,0,1:T(8,128)(2,1)}), bf16[256,4,128]{2,0,1:T(8,128)(2,1)S(1)}, u32[]{:S(2)}, u32[]{:S(2)}) async-start(bf16[256,4,128]{2,0,1:T(8,128)(2,1)} %bitcast.103), calls=%async_computation | async-start | bytes 524288 | tf_op jit(solution)/shard_map/all_to_all | solution.py:105
  17.3 0.0 copy-done.3
  17.3 5.9 %all-to-all-done = bf16[256,4,128]{2,0,1:T(8,128)(2,1)S(1)} async-done(((bf16[256,4,128]{2,0,1:T(8,128)(2,1)}), bf16[256,4,128]{2,0,1:T(8,128)(2,1)S(1)}, u32[]{:S(2)}, u32[]{:S(2)}) %all-to-all-start) | async-done | bytes 262176 | tf_op jit(solution)/shard_map/all_to_all | solution.py:105
  23.3 0.2 copy.24
  23.5 0.2 reshape.165
  23.7 1.0 %fusion.2 = bf16[256,2,3,256]{3,2,0,1:T(4,128)(2,1)S(1)} fusion(bf16[256,2,256,1]{2,1,0,3:T(2,128)(2,1)S(1)} %reshape.165, s32[2,3]{1,0:T(2,128)S(1)} %and_select_fusion), kind=kOutput, calls=%fused_computation.9 | convolution fusion | flops 1966092 | bytes 1048600 | tf_op jit(solution)/shard_map/rsp,jbs->rjbp/dot_general | solution.py:61
  24.7 2.0 %convolution_bitcast_fusion = f32[256,2,3,256]{3,0,2,1:T(8,128)S(1)} fusion(bf16[2,3,256,256]{3,2,1,0:T(8,128)(2,1)} %param.10, bf16[256,2,3,256]{3,2,0,1:T(4,128)(2,1)S(1)} %fusion.2), kind=kOutput, calls=%fused_computation.7 | convolution fusion | flops 402784256 | bytes 3145728 | tf_op jit(solution)/shard_map/rjq,jbpq->rjbp/dot_general | solution.py:67
  26.7 2.9 %fusion.11 = bf16[256,2,256]{2,1,0:T(2,128)(2,1)S(1)} fusion(f32[256,2,3,256]{3,0,2,1:T(8,128)S(1)} %convolution_bitcast_fusion, s32[2,3]{1,0:T(2,128)S(1)} %and_select_fusion), kind=kOutput, calls=%fused_computation.18 | convolution fusion | flops 9568268 | bytes 1835032 | tf_op jit(solution)/shard_map/rjbp,jbs->rsp/dot_general | solution.py:70
  29.6 0.2 convert_element_type.59
  29.8 0.6 %constant_dynamic-slice_fusion.3 = (bf16[256,1,128]{2,1,0:T(2,128)(2,1)S(1)}, bf16[256,1,128]{2,1,0:T(2,128)(2,1)S(1)}, bf16[256,1,128]{2,1,0:T(2,128)(2,1)S(1)}, bf16[256,1,128]{2,1,0:T(2,128)(2,1)S(1)}) fusion(bf16[256,4,128]{2,1,0:T(4,128)(2,1)S(1)} %convert_element_type.59, s32[]{:T(128)S(6)} %select_n.57, s32[]{:T(128)S(6)} %select_n.59, ...), kind=kLoop, calls=%fused_computation.75 | loop fusion | bytes 524304 | tf_op jit(solution)/shard_map/dynamic-slice
  30.4 0.1 collective-permute-start.2
  30.5 0.5 collective-permute-start.3
  31.0 1.5 %collective-permute-start.4 = (bf16[256,128]{1,0:T(8,128)(2,1)S(1)}, bf16[256,128]{1,0:T(8,128)(2,1)S(1)}, u32[]{:S(2)}, u32[]{:S(2)}) collective-permute-start(bf16[256,128]{1,0:T(8,128)(2,1)S(1)} %bitcast.114), channel_id=1, source_target_pairs={{0,3},{1,2},{2,1},{3,0},{4,7},{5,6},{6,5},{7,4},{8,11},{9,10},{10,... | collective-permute-start | bytes 196616 | tf_op jit(solution)/shard_map/ppermute | solution.py:25
  32.5 0.0 collective-permute-done.2
  32.5 3.0 %collective-permute-done.3 = bf16[256,128]{1,0:T(8,128)(2,1)S(1)} collective-permute-done((bf16[256,128]{1,0:T(8,128)(2,1)S(1)}, bf16[256,128]{1,0:T(8,128)(2,1)S(1)}, u32[]{:S(2)}, u32[]{:S(2)}) %collective-permute-start.3) | collective-permute-done | bytes 65568 | tf_op jit(solution)/shard_map/ppermute | solution.py:25
  35.5 0.4 collective-permute-done.4
  36.0 0.6 %gather_fusion = bf16[4,256,128]{2,1,0:T(8,128)(2,1)S(1)} fusion(bf16[4,256,128]{2,1,0:T(8,128)(2,1)S(1)} %pad_maximum_fusion, s32[1024]{0:T(1024)S(1)} %pad_clamp_fusion), kind=kCustom, calls=%fused_computation.2 | custom fusion | bytes 524304 | tf_op jit(solution)/shard_map/gather | solution.py:26
  36.6 0.1 copy.31
  36.8 0.0 copy-start.2
  36.8 0.8 %fusion.47 = (bf16[256,1024]{1,0:T(8,128)(2,1)S(1)}, f32[256,1024]{1,0:T(8,128)S(1)}) fusion(bf16[1024,384]{1,0:T(8,128)(2,1)S(1)} %copy-done, bf16[256,512]{0,1:T(8,128)(2,1)S(1)} %bitcast.109, s32[384]{0:T(512)S(1)} %add_reduce_fusion), kind=kOutput, calls=%fused_computation.81 | convolution fusion | flops 302546944 | bytes 2622976 | tf_op jit(solution)/shard_map/dot_general | solution.py:47
  37.6 0.3 collective-permute-start.5
  37.9 5.0 %collective-permute-start.6 = (bf16[256,128]{1,0:T(8,128)(2,1)S(1)}, bf16[256,128]{1,0:T(8,128)(2,1)S(1)}, u32[]{:S(2)}, u32[]{:S(2)}) collective-permute-start(bf16[256,128]{1,0:T(8,128)(2,1)S(1)} %get-tuple-element.11), channel_id=1, source_target_pairs={{1,0},{2,1},{3,2},{4,3},{5,4},{6,5},{7,6},{8,7},{9,8},{10,9},{11,1... | collective-permute-start | bytes 196616 | tf_op jit(solution)/shard_map/ppermute | solution.py:39
  43.0 0.0 copy-done.2
  43.0 0.1 slice.47
  43.1 0.3 copy.32
  43.3 1.6 %collective-permute-done.5 = bf16[256,128]{1,0:T(8,128)(2,1)S(1)} collective-permute-done((bf16[256,128]{1,0:T(8,128)(2,1)S(1)}, bf16[256,128]{1,0:T(8,128)(2,1)S(1)}, u32[]{:S(2)}, u32[]{:S(2)}) %collective-permute-start.5) | collective-permute-done | bytes 65568 | tf_op jit(solution)/shard_map/ppermute | solution.py:37
  44.9 0.0 collective-permute-done.6
  45.0 0.1 copy.33
  45.1 0.1 copy.34
  45.2 1.6 %scatter_fusion = f32[256,768]{0,1:T(8,128)S(1)} fusion(f32[256,768]{0,1:T(8,128)S(1)} %copy.32, s32[128]{0:T(128)S(1)} %get-tuple-element.19, f32[128,256]{1,0:T(8,128)S(1)} %copy.33), kind=kCustom, calls=%fused_computation.3 | custom fusion | flops 32768 | bytes 393728 | tf_op jit(solution)/shard_map/scatter-add | solution.py:123
  46.8 1.6 %scatter_fusion.1 = f32[256,768]{0,1:T(8,128)S(1)} fusion(f32[256,768]{0,1:T(8,128)S(1)} %scatter_fusion, s32[128]{0:T(128)S(1)} %get-tuple-element.18, f32[128,256]{1,0:T(8,128)S(1)} %copy.34), kind=kCustom, calls=%fused_computation.4 | custom fusion | flops 32768 | bytes 393728 | tf_op jit(solution)/shard_map/scatter-add | solution.py:124
  48.4 1.1 %copy.35 = f32[256,768]{1,0:T(8,128)} copy(f32[256,768]{0,1:T(8,128)S(1)} %scatter_fusion.1) | data formatting | bytes 1572864 | tf_op jit(solution)/shard_map/scatter-add | solution.py:124
  (17 shorter events, 0.2 us)
Async XLA Ops:
  0.0 12.4 %copy-start = (bf16[1024,384]{1,0:T(8,128)(2,1)S(1)}, bf16[1024,384]{1,0:T(8,128)(2,1)}, u32[]{:S(2)}) copy-start(bf16[1024,384]{1,0:T(8,128)(2,1)} %param.9) | copy-start | bytes 2359300
  0.0 10.5 %copy-start.1 = (s32[384,1]{0,1:T(1,128)S(1)}, s32[384,1]{0,1:T(1,128)}, u32[]{:S(2)}) copy-start(s32[384,1]{0,1:T(1,128)} %param.12) | copy-start | bytes 4612
  3.1 9.3 %collective-permute-start = (bf16[256,128]{0,1:T(8,128)(2,1)S(1)}, bf16[256,128]{0,1:T(8,128)(2,1)S(1)}, u32[]{:S(2)}, u32[]{:S(2)}) collective-permute-start(bf16[256,128]{0,1:T(8,128)(2,1)S(1)} %select_bitcast_fusion.1), channel_id=1, source_target_pairs={{0,1},{1,2},{2,3},{3,4},{4,5},{5,6},{6,7},{7,8},{8,9},{9,10},{10,1... | collective-permute-start | bytes 196616 | tf_op jit(solution)/shard_map/ppermute | solution.py:37
  4.5 7.9 %collective-permute-start.1 = (bf16[256,128]{0,1:T(8,128)(2,1)S(1)}, bf16[256,128]{0,1:T(8,128)(2,1)S(1)}, u32[]{:S(2)}, u32[]{:S(2)}) collective-permute-start(bf16[256,128]{0,1:T(8,128)(2,1)S(1)} %select_bitcast_fusion), channel_id=1, source_target_pairs={{1,0},{2,1},{3,2},{4,3},{5,4},{6,5},{7,6},{8,7},{9,8},{10,9},{11,1... | collective-permute-start | bytes 196616 | tf_op jit(solution)/shard_map/ppermute | solution.py:39
  12.3 5.0 %copy-start.3 = (s32[2,3]{1,0:T(2,128)S(1)}, s32[2,3]{1,0:T(2,128)}, u32[]{:S(2)}) copy-start(s32[2,3]{1,0:T(2,128)} %param.11) | copy-start | bytes 76
  13.9 9.4 %all-to-all-start = ((bf16[256,4,128]{2,0,1:T(8,128)(2,1)}), bf16[256,4,128]{2,0,1:T(8,128)(2,1)S(1)}, u32[]{:S(2)}, u32[]{:S(2)}) async-start(bf16[256,4,128]{2,0,1:T(8,128)(2,1)} %bitcast.103), calls=%async_computation | async-start | bytes 524288 | tf_op jit(solution)/shard_map/all_to_all | solution.py:105
  30.4 2.1 %collective-permute-start.2 = (bf16[256,128]{1,0:T(8,128)(2,1)S(1)}, bf16[256,128]{1,0:T(8,128)(2,1)S(1)}, u32[]{:S(2)}, u32[]{:S(2)}) collective-permute-start(bf16[256,128]{1,0:T(8,128)(2,1)S(1)} %bitcast.112), channel_id=1, source_target_pairs={{0,1},{1,0},{2,3},{3,2},{4,5},{5,4},{6,7},{7,6},{8,9},{9,8},{10,11... | collective-permute-start | bytes 196616 | tf_op jit(solution)/shard_map/ppermute | solution.py:25
  30.5 5.0 %collective-permute-start.3 = (bf16[256,128]{1,0:T(8,128)(2,1)S(1)}, bf16[256,128]{1,0:T(8,128)(2,1)S(1)}, u32[]{:S(2)}, u32[]{:S(2)}) collective-permute-start(bf16[256,128]{1,0:T(8,128)(2,1)S(1)} %bitcast.113), channel_id=1, source_target_pairs={{0,2},{1,3},{2,0},{3,1},{4,6},{5,7},{6,4},{7,5},{8,10},{9,11},{10,... | collective-permute-start | bytes 196616 | tf_op jit(solution)/shard_map/ppermute | solution.py:25
  31.0 5.0 %collective-permute-start.4 = (bf16[256,128]{1,0:T(8,128)(2,1)S(1)}, bf16[256,128]{1,0:T(8,128)(2,1)S(1)}, u32[]{:S(2)}, u32[]{:S(2)}) collective-permute-start(bf16[256,128]{1,0:T(8,128)(2,1)S(1)} %bitcast.114), channel_id=1, source_target_pairs={{0,3},{1,2},{2,1},{3,0},{4,7},{5,6},{6,5},{7,4},{8,11},{9,10},{10,... | collective-permute-start | bytes 196616 | tf_op jit(solution)/shard_map/ppermute | solution.py:25
  36.8 6.2 %copy-start.2 = (s32[2,128]{1,0:T(2,128)S(1)}, s32[2,128]{1,0:T(2,128)}, u32[]{:S(2)}) copy-start(s32[2,128]{1,0:T(2,128)} %param.13) | copy-start | bytes 3076
  37.6 7.3 %collective-permute-start.5 = (bf16[256,128]{1,0:T(8,128)(2,1)S(1)}, bf16[256,128]{1,0:T(8,128)(2,1)S(1)}, u32[]{:S(2)}, u32[]{:S(2)}) collective-permute-start(bf16[256,128]{1,0:T(8,128)(2,1)S(1)} %get-tuple-element.10), channel_id=1, source_target_pairs={{0,1},{1,2},{2,3},{3,4},{4,5},{5,6},{6,7},{7,8},{8,9},{9,10},{10,1... | collective-permute-start | bytes 196616 | tf_op jit(solution)/shard_map/ppermute | solution.py:37
  37.9 7.0 %collective-permute-start.6 = (bf16[256,128]{1,0:T(8,128)(2,1)S(1)}, bf16[256,128]{1,0:T(8,128)(2,1)S(1)}, u32[]{:S(2)}, u32[]{:S(2)}) collective-permute-start(bf16[256,128]{1,0:T(8,128)(2,1)S(1)} %get-tuple-element.11), channel_id=1, source_target_pairs={{1,0},{2,1},{3,2},{4,3},{5,4},{6,5},{7,6},{8,7},{9,8},{10,9},{11,1... | collective-permute-start | bytes 196616 | tf_op jit(solution)/shard_map/ppermute | solution.py:39
